TPU v7x, 256 devices: a whole 4x4x8 slice. The times are simulated.
256 devices in a mesh: expert: 8 (over y, core), shard: 32 (over z, x).
Axes of the slice: x: 4, y: 4, z: 8, core: 2. Of those that a mesh axis runs over, the one named last changes fastest.
Arguments:
- master_down: float32 [16, 6400, 4096], P('expert', None, 'shard'), may hold values from -0.15625 to 0.15625
- second_down: bfloat16 [16, 6400, 4096], P('expert', None, 'shard'), may hold values from -0.0390625 to 0.0390625
- router_weight: float32 [4096, 16], P('shard', 'expert'), may hold values from -0.09375 to 0.09375
- router_gain: float32 [4096], P('shard'), may hold values from 0.25 to 1.75
Outputs:
- final_down: bfloat16 [16, 6400, 4096], P('expert', 'shard')
- scale_down: float32 [16, 6400], P('expert', 'shard')
- serve_router: bfloat16 [4096, 16], replicated
All inputs are finite; a program needn't handle non-finite values.
Results may differ from a plain program's by a relative error of at most 0.0085.
Values may be sent and summed in bfloat16 or wider, within the bound.
A program may use at most 64 MiB of HBM per device.

v0:
```python
import jax
import jax.numpy as jnp
from jax import lax
from jax.sharding import PartitionSpec as P


def sent_to_all(x, axis):
    count = lax.axis_size(axis)
    return lax.all_to_all(jnp.broadcast_to(x[None], (count, *x.shape)), axis, 0, 0, tiled=True)


def taken_together(x, axis):
    everything = sent_to_all(x, axis)
    return jnp.sum(everything.astype(jnp.float32), axis=0)


def laid_out(parts, dim):
    dims = list(parts.shape[1:])
    dims[dim] *= parts.shape[0]
    return jnp.moveaxis(parts, 0, dim).reshape(dims)


def gathered_copies(x, axis, dim):
    parts = sent_to_all(x, axis)
    return laid_out(parts, dim)


def body(master_down, second_down, router_weight, router_gain):
    merged_down = master_down + second_down.astype(jnp.float32)
    total_down = taken_together(
        jnp.sum(merged_down * merged_down, axis=2).astype(jnp.bfloat16), "shard"
    ).astype(jnp.float32)
    scale_down = jnp.sqrt(total_down)
    narrow_down = (merged_down / jnp.expand_dims(scale_down, 2)).astype(jnp.bfloat16)
    final_down = lax.all_to_all(narrow_down, "shard", split_axis=1, concat_axis=2, tiled=True)
    scale_down = lax.dynamic_slice_in_dim(
        scale_down, lax.axis_index("shard") * final_down.shape[1], final_down.shape[1], axis=1
    )
    part_router = (router_weight * router_gain[:, None]).astype(jnp.bfloat16)
    row_router = gathered_copies(part_router, "shard", 0)
    serve_router = gathered_copies(row_router, "expert", 1)
    return (final_down, scale_down, serve_router)


def solution(mesh):
    placed = (
        P("expert", None, "shard"),
        P("expert", None, "shard"),
        P("shard", "expert"),
        P("shard"),
    )
    return jax.shard_map(
        body,
        mesh=mesh,
        in_specs=placed,
        out_specs=(P("expert", "shard", None), P("expert", "shard"), P()),
        check_vma=False,
    )
```

profile of v0, /device:TPU:64, one launch (start us, length us, event | category | flops | bytes accessed | tf_op | source)
XLA Modules:
  0.0 180.6 jit_solution(7028451042214102554)
XLA Ops:
  0.6 0.7 multiply_convert_fusion
  1.3 0.6 broadcast_in_dim.9
  1.9 10.7 %all-to-all-start.2 = ((bf16[32,128,2]{1,2,0:T(2,128)(2,1)}), bf16[32,128,2]{1,2,0:T(2,128)(2,1)S(1)}, u32[]{:S(2)}, u32[]{:S(2)}) async-start(bf16[32,128,2]{1,2,0:T(2,128)(2,1)} %broadcast_in_dim.9), calls=%async_computation.2 | async-start | bytes 32768 | tf_op jit(solution)/shard_map/all_to_all | solution.py:9
  12.7 0.0 copy-start
  12.7 5.7 %multiply_reduce_fusion = bf16[2,6400]{1,0:T(2,128)(2,1)S(1)} fusion(f32[2,6400,128]{2,1,0:T(8,128)} %param.4, bf16[2,6400,128]{2,1,0:T(8,128)(2,1)} %param.5), kind=kLoop, calls=%fused_computation.1 | loop fusion | flops 6540800 | bytes 9856000 | tf_op jit(solution)/shard_map/reduce_sum | solution.py:31
  18.4 1.9 %all-to-all-done.2 = bf16[32,128,2]{1,2,0:T(2,128)(2,1)S(1)} async-done(((bf16[32,128,2]{1,2,0:T(2,128)(2,1)}), bf16[32,128,2]{1,2,0:T(2,128)(2,1)S(1)}, u32[]{:S(2)}, u32[]{:S(2)}) %all-to-all-start.2) | async-done | bytes 16416 | tf_op jit(solution)/shard_map/all_to_all | solution.py:9
  20.3 0.4 broadcast_in_dim.8
  20.8 30.5 %all_to_all.33 = bf16[32,2,6400]{2,1,0:T(2,128)(2,1)} all-to-all(bf16[32,2,6400]{2,1,0:T(2,128)(2,1)S(1)} %broadcast_in_dim.8), channel_id=1, replica_groups=mesh['expert'=8,'shard'=32] {'shard'}, dimensions={0} | all-to-all | bytes 1638400 | tf_op jit(solution)/shard_map/all_to_all | solution.py:9
  51.2 0.7 broadcast_in_dim.11
  51.9 4.5 %all-to-all-start.3 = ((bf16[8,4096,2]{1,2,0:T(2,128)(2,1)}), bf16[8,4096,2]{1,2,0:T(2,128)(2,1)S(1)}, u32[]{:S(2)}, u32[]{:S(2)}) async-start(bf16[8,4096,2]{1,2,0:T(2,128)(2,1)} %broadcast_in_dim.11), calls=%async_computation.3 | async-start | bytes 262144 | tf_op jit(solution)/shard_map/all_to_all | solution.py:9
  56.4 1.3 convert_reduce_fusion
  57.8 0.1 sqrt.7
  57.8 0.0 copy-done
  57.8 4.7 %divide_convert_fusion = bf16[2,6400,128]{2,1,0:T(8,128)(2,1)S(1)} fusion(f32[2,6400,128]{2,1,0:T(8,128)} %param.4, bf16[2,6400,128]{2,1,0:T(8,128)(2,1)S(1)} %copy-done, f32[2,6400]{1,0:T(2,128)S(1)} %sqrt.7), kind=kLoop, calls=%fused_computation | loop fusion | flops 6553600 | bytes 13158400 | tf_op jit(solution)/shard_map/convert_element_type | solution.py:34
  62.6 27.9 %copy.31 = bf16[2,6400,128]{2,0,1:T(2,128)(2,1)} copy(bf16[2,6400,128]{2,1,0:T(8,128)(2,1)S(1)} %divide_convert_fusion) | data formatting | bytes 6553600 | tf_op jit(solution)/shard_map/convert_element_type | solution.py:34
  90.5 0.0 all-to-all-done.3
  90.5 5.5 %all-to-all-start.1 = ((bf16[2,6400,128]{2,0,1:T(2,128)(2,1)}), bf16[2,6400,128]{2,0,1:T(2,128)(2,1)S(1)}, u32[]{:S(2)}, u32[]{:S(2)}) async-start(bf16[2,6400,128]{2,0,1:T(2,128)(2,1)} %copy.31), calls=%async_computation.1 | async-start | bytes 6553600 | tf_op jit(solution)/shard_map/all_to_all | solution.py:35
  96.0 0.7 reshape.18
  96.7 0.7 constant_dynamic-slice_fusion
  97.3 74.5 %all-to-all-done.1 = bf16[2,6400,128]{2,0,1:T(2,128)(2,1)S(1)} async-done(((bf16[2,6400,128]{2,0,1:T(2,128)(2,1)}), bf16[2,6400,128]{2,0,1:T(2,128)(2,1)S(1)}, u32[]{:S(2)}, u32[]{:S(2)}) %all-to-all-start.1) | async-done | bytes 3276832 | tf_op jit(solution)/shard_map/all_to_all | solution.py:35
  171.9 2.5 %copy.32 = bf16[2,200,32,128]{3,2,1,0:T(8,128)(2,1)} copy(bf16[2,200,32,128]{3,0,1,2:T(2,128)(2,1)S(1)} %bitcast.9) | data formatting | bytes 6553600 | tf_op jit(solution)/shard_map/all_to_all | solution.py:35
  174.4 6.2 %all_to_all.26 = bf16[2,200,4096]{2,1,0:T(8,128)(2,1)} reshape(bf16[2,200,32,128]{3,2,1,0:T(8,128)(2,1)} %copy.32) | data formatting | bytes 6553600 | tf_op jit(solution)/shard_map/all_to_all | solution.py:35
Async XLA Ops:
  1.9 18.4 %all-to-all-start.2 = ((bf16[32,128,2]{1,2,0:T(2,128)(2,1)}), bf16[32,128,2]{1,2,0:T(2,128)(2,1)S(1)}, u32[]{:S(2)}, u32[]{:S(2)}) async-start(bf16[32,128,2]{1,2,0:T(2,128)(2,1)} %broadcast_in_dim.9), calls=%async_computation.2 | async-start | bytes 32768 | tf_op jit(solution)/shard_map/all_to_all | solution.py:9
  12.7 45.1 %copy-start = (bf16[2,6400,128]{2,1,0:T(8,128)(2,1)S(1)}, bf16[2,6400,128]{2,1,0:T(8,128)(2,1)}, u32[]{:S(2)}) copy-start(bf16[2,6400,128]{2,1,0:T(8,128)(2,1)} %param.5) | copy-start | bytes 9830404
  51.9 38.5 %all-to-all-start.3 = ((bf16[8,4096,2]{1,2,0:T(2,128)(2,1)}), bf16[8,4096,2]{1,2,0:T(2,128)(2,1)S(1)}, u32[]{:S(2)}, u32[]{:S(2)}) async-start(bf16[8,4096,2]{1,2,0:T(2,128)(2,1)} %broadcast_in_dim.11), calls=%async_computation.3 | async-start | bytes 262144 | tf_op jit(solution)/shard_map/all_to_all | solution.py:9
  90.5 81.4 %all-to-all-start.1 = ((bf16[2,6400,128]{2,0,1:T(2,128)(2,1)}), bf16[2,6400,128]{2,0,1:T(2,128)(2,1)S(1)}, u32[]{:S(2)}, u32[]{:S(2)}) async-start(bf16[2,6400,128]{2,0,1:T(2,128)(2,1)} %copy.31), calls=%async_computation.1 | async-start | bytes 6553600 | tf_op jit(solution)/shard_map/all_to_all | solution.py:35
where the time goes:
time: 184 us; the launch traced here: 181 us
  waiting for transfers between devices  76.4 us (42%)
  local copies, waits for them, and re-layouts  39.8 us (22%)
  blocking collectives  30.5 us (17%)
  starting transfers between devices  20.7 us (11%)
  other arithmetic  12.5 us (7%)
    all_to_all x1, waiting for transfers between devices, body(): lax.all_to_all(narrow_down, 'shard', split_axis=1, concat_axis=2, tiled=T...  74.5 us
    all_to_all x1, blocking collectives, sent_to_all(): lax.all_to_all(jnp.broadcast_to(x[None], (count, *x.shape)), axis, 0, 0,...  30.5 us
    convert_element_type x1, local copies, waits for them, and re-layouts, body(): (merged_down / jnp.expand_dims(scale_down, 2)).astype(jnp.bfloat16)  27.9 us
    all_to_all x2, starting transfers between devices, sent_to_all(): lax.all_to_all(jnp.broadcast_to(x[None], (count, *x.shape)), axis, 0, 0,...  15.2 us
    all_to_all x2, local copies, waits for them, and re-layouts, body(): lax.all_to_all(narrow_down, 'shard', split_axis=1, concat_axis=2, tiled=T...  8.72 us
    reduce_sum x1, other arithmetic, body(): jnp.sum(merged_down * merged_down, axis=2).astype(jnp.bfloat16)  5.75 us
    all_to_all x1, starting transfers between devices, body(): lax.all_to_all(narrow_down, 'shard', split_axis=1, concat_axis=2, tiled=T...  5.5 us
    convert_element_type x1, other arithmetic, body(): (merged_down / jnp.expand_dims(scale_down, 2)).astype(jnp.bfloat16)  4.74 us
  transfers between devices with their start and end apart: 3, of which 2 were waited for; matrix products, arithmetic and copies ran while one was open for 23% of the time, Pallas kernels for 0%

commit v1 on v0

v1 whole, which is shorter than its diff:
```python
import jax
import jax.numpy as jnp
from jax import lax
from jax.sharding import PartitionSpec as P


def sent_to_all(x, axis):
    count = lax.axis_size(axis)
    return lax.all_to_all(jnp.broadcast_to(x[None], (count, *x.shape)), axis, 0, 0, tiled=True)


def body(master_down, second_down, router_weight, router_gain):
    shards = lax.axis_size("shard")
    experts, rows, width = master_down.shape
    merged = (master_down + second_down.astype(jnp.float32)).astype(jnp.bfloat16)
    parts = jnp.moveaxis(merged.reshape(experts, shards, rows // shards, width), 1, 0)
    mine = lax.all_to_all(parts, "shard", 0, 0, tiled=True).astype(jnp.float32)
    scale = jnp.sqrt(jnp.sum(mine * mine, axis=(0, 3)))
    final = (mine / scale[None, :, :, None]).astype(jnp.bfloat16)
    final = jnp.moveaxis(final, 0, 2).reshape(experts, rows // shards, shards * width)

    part_router = (router_weight * router_gain[:, None]).astype(jnp.bfloat16).T
    of_shards = sent_to_all(part_router, "shard")
    of_all = sent_to_all(of_shards, "expert")
    serve_router = jnp.transpose(of_all, (1, 3, 0, 2)).reshape(shards * width, -1)
    return (final, scale, serve_router)


def solution(mesh):
    placed = (
        P("expert", None, "shard"),
        P("expert", None, "shard"),
        P("shard", "expert"),
        P("shard"),
    )
    return jax.shard_map(
        body,
        mesh=mesh,
        in_specs=placed,
        out_specs=(P("expert", "shard", None), P("expert", "shard"), P()),
        check_vma=False,
    )
```

time: 184 us -> 120 us (0.65)
  the two profiles are of different devices: /device:TPU:64 before, /device:TPU:7 now
where the time goes in v1:
time: 120 us; the launch traced here: 119 us
  waiting for transfers between devices  76.8 us (64%)
  blocking collectives  17.9 us (15%)
  starting transfers between devices  12 us (10%)
  other arithmetic  8.43 us (7%)
  local copies, waits for them, and re-layouts  3.35 us (3%)
    all_to_all x1, waiting for transfers between devices, body(): mine = lax.all_to_all(parts, 'shard', 0, 0, tiled=True).astype(jnp.float32)  76.8 us
    all_to_all x1, blocking collectives, sent_to_all(): lax.all_to_all(jnp.broadcast_to(x[None], (count, *x.shape)), axis, 0, 0,...  17.9 us
    all_to_all x1, starting transfers between devices, sent_to_all(): lax.all_to_all(jnp.broadcast_to(x[None], (count, *x.shape)), axis, 0, 0,...  6.57 us
    all_to_all x1, starting transfers between devices, body(): mine = lax.all_to_all(parts, 'shard', 0, 0, tiled=True).astype(jnp.float32)  5.47 us
    convert_element_type x1, other arithmetic, body(): (master_down + second_down.astype(jnp.float32)).astype(jnp.bfloat16)  4.44 us
    reshape x1, other arithmetic, body(): jnp.moveaxis(final, 0, 2).reshape(experts, rows // shards, shards * width)  2.58 us
  transfers between devices with their start and end apart: 2, of which 1 were waited for; matrix products, arithmetic and copies ran while one was open for 6% of the time, Pallas kernels for 0%

profile of v1, /device:TPU:7, one launch (start us, length us, event | category | flops | bytes accessed | tf_op | source)
XLA Modules:
  0.0 119.2 jit_solution(7903180785922248613)
XLA Ops:
  0.6 0.7 fusion.3
  1.3 17.9 %all_to_all.15 = bf16[32,2,128]{2,1,0:T(2,128)(2,1)S(1)} all-to-all(bf16[32,2,128]{2,1,0:T(2,128)(2,1)S(1)} %broadcast_in_dim.4), channel_id=1, replica_groups=mesh['expert'=8,'shard'=32] {'shard'}, dimensions={0} | all-to-all | bytes 32768 | tf_op jit(solution)/shard_map/all_to_all | solution.py:9
  19.2 0.7 broadcast_in_dim.5
  19.9 6.6 %all-to-all-start.2 = ((bf16[8,32,2,128]{3,1,2,0:T(8,128)(2,1)}), bf16[8,32,2,128]{3,1,2,0:T(8,128)(2,1)S(1)}, u32[]{:S(2)}, u32[]{:S(2)}) async-start(bf16[8,32,2,128]{3,1,2,0:T(8,128)(2,1)} %broadcast_in_dim.5), calls=%async_computation.2 | async-start | bytes 262144 | tf_op jit(solution)/shard_map/all_to_all | solution.py:9
  26.5 4.4 %add_convert_fusion = bf16[2,6400,128]{2,1,0:T(8,128)(2,1)S(1)} fusion(f32[2,6400,128]{2,1,0:T(8,128)} %param.4, bf16[2,6400,128]{2,1,0:T(8,128)(2,1)} %param.5), kind=kLoop, calls=%fused_computation.4 | loop fusion | flops 4915200 | bytes 13107200 | tf_op jit(solution)/shard_map/convert_element_type | solution.py:15
  30.9 1.9 %copy.9 = bf16[32,2,200,128]{3,2,1,0:T(8,128)(2,1)} copy(bf16[32,2,200,128]{3,2,0,1:T(8,128)(2,1)S(1)} %bitcast.19) | data formatting | bytes 6553600 | tf_op jit(solution)/shard_map/transpose | solution.py:16
  32.9 0.0 all-to-all-done.2
  32.9 5.5 %all-to-all-start = ((bf16[32,2,200,128]{3,2,1,0:T(8,128)(2,1)}), bf16[32,2,200,128]{3,2,1,0:T(8,128)(2,1)S(1)}, u32[]{:S(2)}, u32[]{:S(2)}) async-start(bf16[32,2,200,128]{3,2,1,0:T(8,128)(2,1)} %copy.9), calls=%async_computation | async-start | bytes 6553600 | tf_op jit(solution)/shard_map/all_to_all | solution.py:17
  38.4 0.7 copy.16
  39.1 76.8 %all-to-all-done = bf16[32,2,200,128]{3,2,1,0:T(8,128)(2,1)S(1)} async-done(((bf16[32,2,200,128]{3,2,1,0:T(8,128)(2,1)}), bf16[32,2,200,128]{3,2,1,0:T(8,128)(2,1)S(1)}, u32[]{:S(2)}, u32[]{:S(2)}) %all-to-all-start) | async-done | bytes 3276832 | tf_op jit(solution)/shard_map/all_to_all | solution.py:17
  115.9 0.7 fusion
  116.6 0.0 copy-start
  116.6 2.6 %copy_bitcast_fusion = bf16[2,200,4096]{2,1,0:T(8,128)(2,1)} fusion(bf16[32,2,200,128]{3,2,1,0:T(8,128)(2,1)S(1)} %all-to-all-done, f32[2,200]{1,0:T(2,128)S(1)} %sqrt.7), kind=kLoop, calls=%fused_computation.6 | loop fusion | flops 4915200 | bytes 6555200 | tf_op jit(solution)/shard_map/reshape | solution.py:20
  119.2 0.0 copy-done
  (3 shorter events, 0.0 us)
Async XLA Ops:
  19.9 13.0 %all-to-all-start.2 = ((bf16[8,32,2,128]{3,1,2,0:T(8,128)(2,1)}), bf16[8,32,2,128]{3,1,2,0:T(8,128)(2,1)S(1)}, u32[]{:S(2)}, u32[]{:S(2)}) async-start(bf16[8,32,2,128]{3,1,2,0:T(8,128)(2,1)} %broadcast_in_dim.5), calls=%async_computation.2 | async-start | bytes 262144 | tf_op jit(solution)/shard_map/all_to_all | solution.py:9
  32.9 83.0 %all-to-all-start = ((bf16[32,2,200,128]{3,2,1,0:T(8,128)(2,1)}), bf16[32,2,200,128]{3,2,1,0:T(8,128)(2,1)S(1)}, u32[]{:S(2)}, u32[]{:S(2)}) async-start(bf16[32,2,200,128]{3,2,1,0:T(8,128)(2,1)} %copy.9), calls=%async_computation | async-start | bytes 6553600 | tf_op jit(solution)/shard_map/all_to_all | solution.py:17
  116.6 2.6 %copy-start = (f32[2,200]{1,0:T(2,128)}, f32[2,200]{1,0:T(2,128)S(1)}, u32[]{:S(2)}) copy-start(f32[2,200]{1,0:T(2,128)S(1)} %sqrt.7) | copy-start | bytes 4804

commit v2 on v1

v2 whole, which is shorter than its diff:
```python
import functools
import jax
import jax.numpy as jnp
from jax import lax
from jax.experimental import pallas as pl
from jax.experimental.pallas import tpu as pltpu
from jax.sharding import PartitionSpec as P

MESH = pl.DeviceIdType.MESH
LONG, WIDE = 8, 4
VLIM = 50 << 20
GROUP = 4


def offsets():
    near = lambda step, size: min(step, size - step)
    order = [(along, across) for along in range(LONG) for across in range(WIDE) if (along, across) != (0, 0)]
    return sorted(order, key=lambda s: (near(s[0], LONG) + near(s[1], WIDE), -near(s[0], LONG), s[1], s[0]))


def distance(step):
    return min(step[0], LONG - step[0]) + min(step[1], WIDE - step[1])


def exchange_kernel(order, experts, master, second, weight, gain, blocks, squares, routed,
                    router, wide, narrow, outgoing, in_sem, send_sem, recv_sem, along_sem, across_sem, expert_sem, round_sem):
    me, mine = lax.axis_index("shard"), lax.axis_index("expert")
    z, x = me // WIDE, lax.rem(me, WIDE)
    count = len(order)

    def shard_at(along, across):
        return lax.rem(z + along, LONG) * WIDE + lax.rem(x + across, WIDE)

    def peer(step):
        return shard_at(*order[step])

    def source(step):
        along, across = order[step]
        return shard_at((LONG - along) % LONG, (WIDE - across) % WIDE)

    def other(step):
        return lax.rem(mine + step + 1, experts)

    barrier = pltpu.get_barrier_semaphore()
    for step in range(count):
        pl.semaphore_signal(barrier, inc=1, device_id={"shard": peer(step)}, device_id_type=MESH)
    for step in range(experts - 1):
        pl.semaphore_signal(barrier, inc=1, device_id={"expert": other(step)}, device_id_type=MESH)

    def load(step):
        whom = peer(step) if step < count else me
        return (pltpu.make_async_copy(master.at[:, whom], wide.at[step], in_sem.at[step, 0]),
                pltpu.make_async_copy(second.at[:, whom], narrow.at[step], in_sem.at[step, 1]))

    def send(step, landing):
        return pltpu.make_async_remote_copy(
            src_ref=outgoing.at[step], dst_ref=blocks.at[landing], send_sem=send_sem.at[step],
            recv_sem=recv_sem.at[step], device_id={"shard": peer(step)}, device_id_type=MESH)

    def merge(step):
        for copy in load(step):
            copy.wait()
        return (wide[step] + narrow[step].astype(jnp.float32)).astype(jnp.bfloat16)

    def along_copy(step, landing):
        return pltpu.make_async_remote_copy(
            src_ref=router.at[mine, z, x], dst_ref=router.at[mine, landing, x], send_sem=along_sem.at[step, 0],
            recv_sem=along_sem.at[step, 1], device_id={"shard": shard_at(step + 1, 0)}, device_id_type=MESH)

    def across_copy(step, landing):
        return pltpu.make_async_remote_copy(
            src_ref=router.at[mine, :, x], dst_ref=router.at[mine, :, landing], send_sem=across_sem.at[step, 0],
            recv_sem=across_sem.at[step, 1], device_id={"shard": shard_at(0, step + 1)}, device_id_type=MESH)

    def expert_copy(step, landing):
        return pltpu.make_async_remote_copy(
            src_ref=router.at[mine], dst_ref=router.at[landing], send_sem=expert_sem.at[step, 0],
            recv_sem=expert_sem.at[step, 1], device_id={"expert": other(step)}, device_id_type=MESH)

    def before(index, step, size):
        return lax.rem(index + size - step - 1, size)

    for step in range(count + 1):
        for copy in load(step):
            copy.start()
    router[mine, z, x] = (weight[...] * gain[...]).astype(jnp.bfloat16)
    first = 4
    for step in range(first):
        outgoing[step] = merge(step)

    pl.semaphore_wait(barrier, count + experts - 1)

    for step in range(LONG - 1):
        along_copy(step, z).start()
    for step in range(first):
        send(step, me).start()
    for step in range(first, 13):
        outgoing[step] = merge(step)
    for step in range(first, 13):
        send(step, me).start()
    for step in range(13, count):
        outgoing[step] = merge(step)
    for step in range(LONG - 1):
        along_copy(step, before(z, step, LONG)).wait_recv()
    for step in range(WIDE - 1):
        across_copy(step, x).start()
    for step in range(13, count):
        send(step, me).start()
    own = merge(count)
    blocks[me] = own
    own = own.astype(jnp.float32)
    squares[...] = own * own
    for step in range(WIDE - 1):
        across_copy(step, before(x, step, WIDE)).wait_recv()
    for step in range(experts - 1):
        expert_copy(step, mine).start()

    for step in range(count):
        if step == count // 2:
            for turn in range(experts - 1):
                expert_copy(turn, before(mine, turn, experts)).wait_recv()
            for along in range(LONG):
                for across in range(WIDE):
                    start = (along * WIDE + across) * 128
                    routed[:, start:start + 128] = router[:, along, across].astype(jnp.float32).reshape(routed.shape[0], 128).astype(jnp.bfloat16)
        send(step, source(step)).wait_recv()
        part = blocks[source(step)].astype(jnp.float32)
        squares[...] += part * part

    for step in range(count):
        send(step, me).wait_send()
    for step in range(LONG - 1):
        along_copy(step, z).wait_send()
    for step in range(WIDE - 1):
        across_copy(step, x).wait_send()
    for step in range(experts - 1):
        expert_copy(step, mine).wait_send()


def exchange(master, second, weight, gain, order):
    held, shards, rows, width = master.shape
    experts = lax.axis_size("expert")
    count = len(order)
    vmem, hbm = pl.BlockSpec(memory_space=pltpu.VMEM), pl.BlockSpec(memory_space=pltpu.MemorySpace.HBM)
    dma = pltpu.SemaphoreType.DMA
    return pl.pallas_call(
        functools.partial(exchange_kernel, order, experts),
        out_shape=(
            jax.ShapeDtypeStruct((shards, held, rows, width), jnp.bfloat16),
            jax.ShapeDtypeStruct((held, rows, width), jnp.float32),
            jax.ShapeDtypeStruct((experts * held, shards * width), jnp.bfloat16),
        ),
        in_specs=[hbm, hbm, vmem, vmem],
        out_specs=(vmem, vmem, vmem),
        scratch_shapes=[
            pltpu.VMEM((experts, LONG, WIDE, held, width), jnp.bfloat16),
            pltpu.VMEM((shards, held, rows, width), jnp.float32),
            pltpu.VMEM((shards, held, rows, width), jnp.bfloat16),
            pltpu.VMEM((count, held, rows, width), jnp.bfloat16),
            dma((shards, 2)), dma((count,)), dma((count,)), dma((LONG - 1, 2)), dma((WIDE - 1, 2)),
            dma((experts - 1, 2)), pltpu.SemaphoreType.REGULAR((8,)),
        ],
        compiler_params=pltpu.CompilerParams(collective_id=0, has_side_effects=True, vmem_limit_bytes=VLIM),
    )(master, second, weight, gain)


def finish_kernel(blocks, squares, routed, final, scale, serve, ready, sem):
    held, rows, width = squares.shape
    copies = [pltpu.make_async_copy(routed, serve, sem.at[0])]
    copies[0].start()
    by_lane = jnp.stack([jnp.sum(jnp.swapaxes(squares[e], 0, 1), axis=0) for e in range(held)])
    scale[...] = jnp.sqrt(by_lane)
    inverse = [1.0 / jnp.sqrt(jnp.sum(squares[e], axis=1, keepdims=True)) for e in range(held)]
    for e in range(held):
        squares[e] = jnp.broadcast_to(inverse[e], (rows, width))
    for start in range(0, blocks.shape[0], GROUP):
        for shard in range(start, start + GROUP):
            ready[:, :, shard * width:(shard + 1) * width] = (
                blocks[shard].astype(jnp.float32) * squares[...]).astype(jnp.bfloat16)
        lanes = pl.ds(start * width, GROUP * width)
        copies.append(pltpu.make_async_copy(ready.at[:, :, lanes], final.at[:, :, lanes], sem.at[len(copies)]))
        copies[-1].start()
    for copy in copies:
        copy.wait()


def finish(blocks, squares, routed):
    shards, held, rows, width = blocks.shape
    vmem, hbm = pl.BlockSpec(memory_space=pltpu.VMEM), pl.BlockSpec(memory_space=pl.ANY)
    return pl.pallas_call(
        finish_kernel,
        out_shape=(
            jax.ShapeDtypeStruct((held, rows, shards * width), jnp.bfloat16),
            jax.ShapeDtypeStruct((held, rows), jnp.float32),
            jax.ShapeDtypeStruct(routed.shape, jnp.bfloat16),
        ),
        in_specs=[vmem, vmem, vmem],
        out_specs=(hbm, vmem, hbm),
        scratch_shapes=[
            pltpu.VMEM((held, rows, shards * width), jnp.bfloat16),
            pltpu.SemaphoreType.DMA((1 + shards // GROUP,)),
        ],
        compiler_params=pltpu.CompilerParams(vmem_limit_bytes=VLIM),
    )(blocks, squares, routed)


def body(master_down, second_down, router_weight, router_gain):
    shards = lax.axis_size("shard")
    held, rows, width = master_down.shape
    cut = (held, shards, rows // shards, width)
    gathered = exchange(
        master_down.reshape(cut), second_down.reshape(cut), router_weight.T, router_gain[None, :], offsets())
    final, scale, serve_router = finish(*gathered)
    return (final, scale, serve_router.T)


def solution(mesh):
    placed = (
        P("expert", None, "shard"),
        P("expert", None, "shard"),
        P("shard", "expert"),
        P("shard"),
    )
    return jax.shard_map(
        body,
        mesh=mesh,
        in_specs=placed,
        out_specs=(P("expert", "shard", None), P("expert", "shard"), P()),
        check_vma=False,
    )
```

time: 120 us -> 90.1 us (0.75)
  the two profiles are of different devices: /device:TPU:7 before, /device:TPU:64 now
where the time goes in v2:
time: 90.1 us; the launch traced here: 89 us
  Pallas kernels  87.1 us (97%)
  local copies, waits for them, and re-layouts  1.33 us (1%)
    pallas_call x1, Pallas kernels, exchange(): pl.pallas_call(functools.partial(exchange_kernel, order, experts), out_sh...  84.1 us
    pallas_call x1, Pallas kernels, finish(): pl.pallas_call(finish_kernel, out_shape=(jax.ShapeDtypeStruct((held, rows...  2.98 us

profile of v2, /device:TPU:64, one launch (start us, length us, event | category | flops | bytes accessed | tf_op | source)
XLA Modules:
  0.0 89.0 jit_solution(1457369590075827191)
XLA Ops:
  0.6 0.0 copy-start
  0.6 0.7 copy-done
  1.3 0.0 copy-start.1
  1.3 0.7 copy-done.1
  2.0 84.1 %shard_map.67 = (bf16[32,2,200,128]{3,2,1,0:T(8,128)(2,1)S(1)}, f32[2,200,128]{2,1,0:T(8,128)S(1)}, bf16[16,4096]{1,0:T(8,128)(2,1)S(1)}) custom-call(f32[2,32,200,128]{3,2,1,0:T(8,128)} %bitcast.7, bf16[2,32,200,128]{3,2,1,0:T(8,128)(2,1)} %bitcast.8, f32[2,128]{1,0:T(2,128)S(1)} %bitcast.5, f32[1,128]{1,0:T(1,128)S(1)} %bitcast.6), custom_call_target="tpu_custom_call" | custom-call | tf_op jit(solution)/shard_map/pallas_call | solution.py:146
  86.1 3.0 %shard_map.68 = (bf16[2,200,4096]{2,1,0:T(8,128)(2,1)}, f32[2,200]{1,0:T(2,128)}, bf16[16,4096]{1,0:T(8,128)(2,1)}) custom-call(bf16[32,2,200,128]{3,2,1,0:T(8,128)(2,1)S(1)} %get-tuple-element.9.blocks, f32[2,200,128]{2,1,0:T(8,128)S(1)} %get-tuple-element.10.squares, bf16[16,4096]{1,0:T(8,128)(2,1)S(1)} %get-tuple-element.11.routed), custom_call_target="tpu_custom_call" | custom-call | tf_op jit(solution)/shard_map/pallas_call | solution.py:190
Async XLA Ops:
  0.6 0.7 copy-start
  1.3 0.7 copy-start.1

commit v3 on v2

--- a/solution.py
+++ b/solution.py
@@ -10,22 +10,23 @@
 LONG, WIDE = 8, 4
 VLIM = 50 << 20
 GROUP = 4
-
-
-def offsets():
+ROUNDS = LONG // 2 + WIDE // 2 - 1
+
+
+def plan():
     near = lambda step, size: min(step, size - step)
-    order = [(along, across) for along in range(LONG) for across in range(WIDE) if (along, across) != (0, 0)]
-    return sorted(order, key=lambda s: (near(s[0], LONG) + near(s[1], WIDE), -near(s[0], LONG), s[1], s[0]))
-
-
-def distance(step):
-    return min(step[0], LONG - step[0]) + min(step[1], WIDE - step[1])
-
-
-def exchange_kernel(order, experts, master, second, weight, gain, blocks, squares, routed,
+    early = [[(1, 0), (LONG - 1, 0), (0, 1), (0, WIDE - 1)], [(2, 0), (LONG - 2, 0)], [(3, 0), (LONG - 3, 0)]]
+    used = [step for group in early for step in group] + [(0, 0)]
+    rest = [(along, across) for along in range(LONG) for across in range(WIDE) if (along, across) not in used]
+    rest.sort(key=lambda s: (-near(s[0], LONG) - near(s[1], WIDE), -near(s[0], LONG), s[1], s[0]))
+    return early + [[]] * (ROUNDS - len(early)) + [rest]
+
+
+def exchange_kernel(plan, experts, master, second, part, blocks, squares, routed,
                     router, wide, narrow, outgoing, in_sem, send_sem, recv_sem, along_sem, across_sem, expert_sem, round_sem):
     me, mine = lax.axis_index("shard"), lax.axis_index("expert")
     z, x = me // WIDE, lax.rem(me, WIDE)
+    order = [step for group in plan for step in group]
     count = len(order)
 
     def shard_at(along, across):
@@ -41,11 +42,20 @@
     def other(step):
         return lax.rem(mine + step + 1, experts)
 
-    barrier = pltpu.get_barrier_semaphore()
-    for step in range(count):
-        pl.semaphore_signal(barrier, inc=1, device_id={"shard": peer(step)}, device_id_type=MESH)
-    for step in range(experts - 1):
-        pl.semaphore_signal(barrier, inc=1, device_id={"expert": other(step)}, device_id_type=MESH)
+    def greet(turn):
+        semaphore = pltpu.get_barrier_semaphore() if turn == 1 else round_sem.at[turn - 2]
+        for along, across in ((1, 0), (LONG - 1, 0), (0, 1), (0, WIDE - 1)):
+            pl.semaphore_signal(semaphore, inc=1, device_id={"shard": shard_at(along, across)}, device_id_type=MESH)
+        if turn <= 3:
+            for near in around:
+                pl.semaphore_signal(semaphore, inc=1, device_id={"expert": near}, device_id_type=MESH)
+
+    def greeted(turn):
+        semaphore = pltpu.get_barrier_semaphore() if turn == 1 else round_sem.at[turn - 2]
+        pl.semaphore_wait(semaphore, 7 if turn <= 3 else 4)
+
+    around = (mine + 1 - 2 * lax.rem(mine, 2), lax.rem(mine + 2, experts), lax.rem(mine + experts - 2, experts))
+    greet(1)
 
     def load(step):
         whom = peer(step) if step < count else me
@@ -83,29 +93,28 @@
     for step in range(count + 1):
         for copy in load(step):
             copy.start()
-    router[mine, z, x] = (weight[...] * gain[...]).astype(jnp.bfloat16)
-    first = 4
-    for step in range(first):
+
+    bounds = [sum(len(group) for group in plan[:turn]) for turn in range(ROUNDS + 2)]
+    for step in range(bounds[1]):
         outgoing[step] = merge(step)
-
-    pl.semaphore_wait(barrier, count + experts - 1)
-
-    for step in range(LONG - 1):
-        along_copy(step, z).start()
-    for step in range(first):
-        send(step, me).start()
-    for step in range(first, 13):
-        outgoing[step] = merge(step)
-    for step in range(first, 13):
-        send(step, me).start()
-    for step in range(13, count):
-        outgoing[step] = merge(step)
+    for turn in range(1, ROUNDS + 2):
+        greeted(turn)
+        if turn <= ROUNDS:
+            greet(turn + 1)
+        if turn == LONG // 2:
+            for step in range(LONG - 1):
+                along_copy(step, z).start()
+        for step in range(bounds[turn - 1], bounds[turn]):
+            send(step, me).start()
+        if turn == 1:
+            router[mine, z, x] = part[...]
+        if turn <= ROUNDS:
+            for step in range(bounds[turn], bounds[turn + 1]):
+                outgoing[step] = merge(step)
     for step in range(LONG - 1):
         along_copy(step, before(z, step, LONG)).wait_recv()
     for step in range(WIDE - 1):
         across_copy(step, x).start()
-    for step in range(13, count):
-        send(step, me).start()
     own = merge(count)
     blocks[me] = own
     own = own.astype(jnp.float32)
@@ -137,20 +146,20 @@
         expert_copy(step, mine).wait_send()
 
 
-def exchange(master, second, weight, gain, order):
+def exchange(master, second, part, plan):
     held, shards, rows, width = master.shape
     experts = lax.axis_size("expert")
-    count = len(order)
+    count = shards - 1
     vmem, hbm = pl.BlockSpec(memory_space=pltpu.VMEM), pl.BlockSpec(memory_space=pltpu.MemorySpace.HBM)
     dma = pltpu.SemaphoreType.DMA
     return pl.pallas_call(
-        functools.partial(exchange_kernel, order, experts),
+        functools.partial(exchange_kernel, plan, experts),
         out_shape=(
             jax.ShapeDtypeStruct((shards, held, rows, width), jnp.bfloat16),
             jax.ShapeDtypeStruct((held, rows, width), jnp.float32),
             jax.ShapeDtypeStruct((experts * held, shards * width), jnp.bfloat16),
         ),
-        in_specs=[hbm, hbm, vmem, vmem],
+        in_specs=[hbm, hbm, vmem],
         out_specs=(vmem, vmem, vmem),
         scratch_shapes=[
             pltpu.VMEM((experts, LONG, WIDE, held, width), jnp.bfloat16),
@@ -158,28 +167,26 @@
             pltpu.VMEM((shards, held, rows, width), jnp.bfloat16),
             pltpu.VMEM((count, held, rows, width), jnp.bfloat16),
             dma((shards, 2)), dma((count,)), dma((count,)), dma((LONG - 1, 2)), dma((WIDE - 1, 2)),
-            dma((experts - 1, 2)), pltpu.SemaphoreType.REGULAR((8,)),
+            dma((experts - 1, 2)), pltpu.SemaphoreType.REGULAR((ROUNDS,)),
         ],
         compiler_params=pltpu.CompilerParams(collective_id=0, has_side_effects=True, vmem_limit_bytes=VLIM),
-    )(master, second, weight, gain)
-
-
-def finish_kernel(blocks, squares, routed, final, scale, serve, ready, sem):
+    )(master, second, part)
+
+
+def finish_kernel(blocks, squares, routed, final, scale, serve, ready, inverse, sem):
     held, rows, width = squares.shape
     copies = [pltpu.make_async_copy(routed, serve, sem.at[0])]
     copies[0].start()
-    by_lane = jnp.stack([jnp.sum(jnp.swapaxes(squares[e], 0, 1), axis=0) for e in range(held)])
-    scale[...] = jnp.sqrt(by_lane)
-    inverse = [1.0 / jnp.sqrt(jnp.sum(squares[e], axis=1, keepdims=True)) for e in range(held)]
     for e in range(held):
-        squares[e] = jnp.broadcast_to(inverse[e], (rows, width))
+        inverse[e] = jnp.broadcast_to(1.0 / jnp.sqrt(jnp.sum(squares[e], axis=1, keepdims=True)), (rows, width))
     for start in range(0, blocks.shape[0], GROUP):
         for shard in range(start, start + GROUP):
             ready[:, :, shard * width:(shard + 1) * width] = (
-                blocks[shard].astype(jnp.float32) * squares[...]).astype(jnp.bfloat16)
+                blocks[shard].astype(jnp.float32) * inverse[...]).astype(jnp.bfloat16)
         lanes = pl.ds(start * width, GROUP * width)
         copies.append(pltpu.make_async_copy(ready.at[:, :, lanes], final.at[:, :, lanes], sem.at[len(copies)]))
         copies[-1].start()
+    scale[...] = jnp.sqrt(jnp.stack([jnp.sum(jnp.swapaxes(squares[e], 0, 1), axis=0) for e in range(held)]))
     for copy in copies:
         copy.wait()
 
@@ -198,6 +205,7 @@
         out_specs=(hbm, vmem, hbm),
         scratch_shapes=[
             pltpu.VMEM((held, rows, shards * width), jnp.bfloat16),
+            pltpu.VMEM((held, rows, width), jnp.float32),
             pltpu.SemaphoreType.DMA((1 + shards // GROUP,)),
         ],
         compiler_params=pltpu.CompilerParams(vmem_limit_bytes=VLIM),
@@ -209,7 +217,7 @@
     held, rows, width = master_down.shape
     cut = (held, shards, rows // shards, width)
     gathered = exchange(
-        master_down.reshape(cut), second_down.reshape(cut), router_weight.T, router_gain[None, :], offsets())
+        master_down.reshape(cut), second_down.reshape(cut), (router_weight.T * router_gain).astype(jnp.bfloat16), plan())
     final, scale, serve_router = finish(*gathered)
     return (final, scale, serve_router.T)
 

time: 90.1 us -> 86.9 us (0.964)
  the two profiles are of different devices: /device:TPU:64 before, /device:TPU:2 now
where the time goes in v3:
time: 86.9 us; the launch traced here: 86.8 us
  Pallas kernels  85.4 us (98%)
    pallas_call x1, Pallas kernels, exchange(): pl.pallas_call(functools.partial(exchange_kernel, plan, experts), out_sha...  82.7 us
    pallas_call x1, Pallas kernels, finish(): pl.pallas_call(finish_kernel, out_shape=(jax.ShapeDtypeStruct((held, rows...  2.71 us

profile of v3, /device:TPU:2, one launch (start us, length us, event | category | flops | bytes accessed | tf_op | source)
XLA Modules:
  0.0 86.8 jit_solution(14853515227573336156)
XLA Ops:
  0.6 0.7 fusion.part
  1.3 82.7 %shard_map.67 = (bf16[32,2,200,128]{3,2,1,0:T(8,128)(2,1)S(1)}, f32[2,200,128]{2,1,0:T(8,128)S(1)}, bf16[16,4096]{1,0:T(8,128)(2,1)S(1)}) custom-call(f32[2,32,200,128]{3,2,1,0:T(8,128)} %bitcast.5, bf16[2,32,200,128]{3,2,1,0:T(8,128)(2,1)} %bitcast.6, bf16[2,128]{1,0:T(2,128)(2,1)S(1)} %fusion.part), custom_call_target="tpu_custom_call" | custom-call | tf_op jit(solution)/shard_map/pallas_call | solution.py:155
  84.1 2.7 %shard_map.68 = (bf16[2,200,4096]{2,1,0:T(8,128)(2,1)}, f32[2,200]{1,0:T(2,128)}, bf16[16,4096]{1,0:T(8,128)(2,1)}) custom-call(bf16[32,2,200,128]{3,2,1,0:T(8,128)(2,1)S(1)} %get-tuple-element.9.blocks, f32[2,200,128]{2,1,0:T(8,128)S(1)} %get-tuple-element.10.squares, bf16[16,4096]{1,0:T(8,128)(2,1)S(1)} %get-tuple-element.11.routed), custom_call_target="tpu_custom_call" | custom-call | tf_op jit(solution)/shard_map/pallas_call | solution.py:197

commit v4 on v3

--- a/solution.py
+++ b/solution.py
@@ -11,33 +11,53 @@
 VLIM = 50 << 20
 GROUP = 4
 ROUNDS = LONG // 2 + WIDE // 2 - 1
+RANKED = {(LONG - 1, 0): 2.5, (LONG - 1, 1): 2, (LONG - 1, 2): 1.5}
 
 
 def plan():
-    near = lambda step, size: min(step, size - step)
-    early = [[(1, 0), (LONG - 1, 0), (0, 1), (0, WIDE - 1)], [(2, 0), (LONG - 2, 0)], [(3, 0), (LONG - 3, 0)]]
-    used = [step for group in early for step in group] + [(0, 0)]
-    rest = [(along, across) for along in range(LONG) for across in range(WIDE) if (along, across) not in used]
-    rest.sort(key=lambda s: (-near(s[0], LONG) - near(s[1], WIDE), -near(s[0], LONG), s[1], s[0]))
-    return early + [[]] * (ROUNDS - len(early)) + [rest]
-
-
-def exchange_kernel(plan, experts, master, second, part, blocks, squares, routed,
-                    router, wide, narrow, outgoing, in_sem, send_sem, recv_sem, along_sem, across_sem, expert_sem, round_sem):
+    early = [[(step, 0), (LONG - step, 0)] for step in range(1, LONG // 2)]
+    sizes = [len(group) for group in early] + [0] * (ROUNDS - len(early))
+    early = [step for group in early for step in group]
+    every = [(along, across) for along in range(LONG) for across in range(WIDE) if (along, across) != (0, 0)]
+
+    def order_at(z):
+        def key(step):
+            along, across = step
+            target = (z + along) % LONG
+            far = RANKED.get((z, target), min(along, LONG - along))
+            other_half = z < LONG // 2 <= target and along != LONG // 2
+            turned = (along > LONG // 2) != (across == WIDE - 1)
+            return other_half, -(far + 2 * min(across, WIDE - across)), -far, turned, across, along
+
+        return early + sorted((step for step in every if step not in early), key=key)
+
+    orders = [order_at(z) for z in range(LONG)]
+    arrivals = [sorted(every, key=lambda step: orders[(z - step[0]) % LONG].index(step)) for z in range(LONG)]
+    return orders, sizes + [len(every) - len(early)], arrivals
+
+
+def exchange_kernel(plan, experts, master, second, weight, gain, blocks, squares, routed,
+                    router, part, scales, wide, narrow, outgoing, in_sem, send_sem, recv_sem, along_sem, across_sem, expert_sem, part_sem, round_sem):
     me, mine = lax.axis_index("shard"), lax.axis_index("expert")
     z, x = me // WIDE, lax.rem(me, WIDE)
-    order = [step for group in plan for step in group]
-    count = len(order)
+    orders, sizes, arrivals = plan
+    count = len(orders[0])
+
+    def chosen(tables, step):
+        along, across = tables[0][step]
+        for place in range(1, LONG):
+            along = jnp.where(z == place, tables[place][step][0], along)
+            across = jnp.where(z == place, tables[place][step][1], across)
+        return along, across
 
     def shard_at(along, across):
         return lax.rem(z + along, LONG) * WIDE + lax.rem(x + across, WIDE)
 
     def peer(step):
-        return shard_at(*order[step])
-
-    def source(step):
-        along, across = order[step]
-        return shard_at((LONG - along) % LONG, (WIDE - across) % WIDE)
+        return shard_at(*chosen(orders, step))
+
+    def code(along, across):
+        return along * WIDE + across
 
     def other(step):
         return lax.rem(mine + step + 1, experts)
@@ -55,8 +75,6 @@
         pl.semaphore_wait(semaphore, 7 if turn <= 3 else 4)
 
     around = (mine + 1 - 2 * lax.rem(mine, 2), lax.rem(mine + 2, experts), lax.rem(mine + experts - 2, experts))
-    greet(1)
-
     def load(step):
         whom = peer(step) if step < count else me
         return (pltpu.make_async_copy(master.at[:, whom], wide.at[step], in_sem.at[step, 0]),
@@ -65,7 +83,14 @@
     def send(step, landing):
         return pltpu.make_async_remote_copy(
             src_ref=outgoing.at[step], dst_ref=blocks.at[landing], send_sem=send_sem.at[step],
-            recv_sem=recv_sem.at[step], device_id={"shard": peer(step)}, device_id_type=MESH)
+            recv_sem=recv_sem.at[code(*chosen(orders, step))], device_id={"shard": peer(step)}, device_id_type=MESH)
+
+    def arrival(step):
+        along, across = chosen(arrivals, step)
+        source = shard_at(LONG - along, WIDE - across)
+        return source, pltpu.make_async_remote_copy(
+            src_ref=outgoing.at[step], dst_ref=blocks.at[source], send_sem=send_sem.at[step],
+            recv_sem=recv_sem.at[code(along, across)], device_id={"shard": source}, device_id_type=MESH)
 
     def merge(step):
         for copy in load(step):
@@ -90,11 +115,18 @@
     def before(index, step, size):
         return lax.rem(index + size - step - 1, size)
 
-    for step in range(count + 1):
-        for copy in load(step):
-            copy.start()
-
-    bounds = [sum(len(group) for group in plan[:turn]) for turn in range(ROUNDS + 2)]
+    def loads(first, last):
+        for step in range(first, last):
+            for copy in load(step):
+                copy.start()
+
+
+    bounds = [sum(sizes[:turn]) for turn in range(ROUNDS + 2)]
+    greet(1)
+    loads(0, bounds[3])
+    pieces = (pltpu.make_async_copy(weight, part, part_sem.at[0]), pltpu.make_async_copy(gain, scales, part_sem.at[1]))
+    for copy in pieces:
+        copy.start()
     for step in range(bounds[1]):
         outgoing[step] = merge(step)
     for turn in range(1, ROUNDS + 2):
@@ -107,7 +139,10 @@
         for step in range(bounds[turn - 1], bounds[turn]):
             send(step, me).start()
         if turn == 1:
-            router[mine, z, x] = part[...]
+            loads(bounds[3], count + 1)
+            for copy in pieces:
+                copy.wait()
+            router[mine, z, x] = (part[...] * scales[...]).astype(jnp.bfloat16)
         if turn <= ROUNDS:
             for step in range(bounds[turn], bounds[turn + 1]):
                 outgoing[step] = merge(step)
@@ -132,8 +167,9 @@
                 for across in range(WIDE):
                     start = (along * WIDE + across) * 128
                     routed[:, start:start + 128] = router[:, along, across].astype(jnp.float32).reshape(routed.shape[0], 128).astype(jnp.bfloat16)
-        send(step, source(step)).wait_recv()
-        part = blocks[source(step)].astype(jnp.float32)
+        source, copy = arrival(step)
+        copy.wait_recv()
+        part = blocks[source].astype(jnp.float32)
         squares[...] += part * part
 
     for step in range(count):
@@ -146,7 +182,7 @@
         expert_copy(step, mine).wait_send()
 
 
-def exchange(master, second, part, plan):
+def exchange(master, second, weight, gain, plan):
     held, shards, rows, width = master.shape
     experts = lax.axis_size("expert")
     count = shards - 1
@@ -159,18 +195,20 @@
             jax.ShapeDtypeStruct((held, rows, width), jnp.float32),
             jax.ShapeDtypeStruct((experts * held, shards * width), jnp.bfloat16),
         ),
-        in_specs=[hbm, hbm, vmem],
+        in_specs=[hbm] * 4,
         out_specs=(vmem, vmem, vmem),
         scratch_shapes=[
             pltpu.VMEM((experts, LONG, WIDE, held, width), jnp.bfloat16),
+            pltpu.VMEM((held, width), jnp.float32),
+            pltpu.VMEM((1, width), jnp.float32),
             pltpu.VMEM((shards, held, rows, width), jnp.float32),
             pltpu.VMEM((shards, held, rows, width), jnp.bfloat16),
             pltpu.VMEM((count, held, rows, width), jnp.bfloat16),
-            dma((shards, 2)), dma((count,)), dma((count,)), dma((LONG - 1, 2)), dma((WIDE - 1, 2)),
-            dma((experts - 1, 2)), pltpu.SemaphoreType.REGULAR((ROUNDS,)),
+            dma((shards, 2)), dma((count,)), dma((shards,)), dma((LONG - 1, 2)), dma((WIDE - 1, 2)),
+            dma((experts - 1, 2)), dma((2,)), pltpu.SemaphoreType.REGULAR((ROUNDS,)),
         ],
         compiler_params=pltpu.CompilerParams(collective_id=0, has_side_effects=True, vmem_limit_bytes=VLIM),
-    )(master, second, part)
+    )(master, second, weight, gain)
 
 
 def finish_kernel(blocks, squares, routed, final, scale, serve, ready, inverse, sem):
@@ -217,7 +255,8 @@
     held, rows, width = master_down.shape
     cut = (held, shards, rows // shards, width)
     gathered = exchange(
-        master_down.reshape(cut), second_down.reshape(cut), (router_weight.T * router_gain).astype(jnp.bfloat16), plan())
+        *(pltpu.with_memory_space_constraint(value, pltpu.HBM) for value in (
+            master_down.reshape(cut), second_down.reshape(cut), router_weight.T, router_gain[None, :])), plan())
     final, scale, serve_router = finish(*gathered)
     return (final, scale, serve_router.T)
 

time: 86.9 us -> 85 us (0.978)
  the two profiles are of different devices: /device:TPU:2 before, /device:TPU:64 now
where the time goes in v4:
time: 85 us; the launch traced here: 84.9 us
  Pallas kernels  84.3 us (99%)
    pallas_call x1, Pallas kernels, exchange(): pl.pallas_call(functools.partial(exchange_kernel, plan, experts), out_sha...  81.6 us
    pallas_call x1, Pallas kernels, finish(): pl.pallas_call(finish_kernel, out_shape=(jax.ShapeDtypeStruct((held, rows...  2.71 us

profile of v4, /device:TPU:64, one launch (start us, length us, event | category | flops | bytes accessed | tf_op | source)
XLA Modules:
  0.0 84.9 jit_solution(17397511895400620255)
XLA Ops:
  0.6 81.6 %shard_map.67 = (bf16[32,2,200,128]{3,2,1,0:T(8,128)(2,1)S(1)}, f32[2,200,128]{2,1,0:T(8,128)S(1)}, bf16[16,4096]{1,0:T(8,128)(2,1)S(1)}) custom-call(f32[2,32,200,128]{3,2,1,0:T(8,128)} %bitcast.5, bf16[2,32,200,128]{3,2,1,0:T(8,128)(2,1)} %bitcast.6, f32[2,128]{1,0:T(2,128)} %bitcast.7, f32[1,128]{1,0:T(1,128)} %bitcast.8), custom_call_target="tpu_custom_call" | custom-call | tf_op jit(solution)/shard_map/pallas_call | solution.py:191
  82.2 2.7 %shard_map.68 = (bf16[2,200,4096]{2,1,0:T(8,128)(2,1)}, f32[2,200]{1,0:T(2,128)}, bf16[16,4096]{1,0:T(8,128)(2,1)}) custom-call(bf16[32,2,200,128]{3,2,1,0:T(8,128)(2,1)S(1)} %get-tuple-element.9.blocks, f32[2,200,128]{2,1,0:T(8,128)S(1)} %get-tuple-element.10.squares, bf16[16,4096]{1,0:T(8,128)(2,1)S(1)} %get-tuple-element.11.routed), custom_call_target="tpu_custom_call" | custom-call | tf_op jit(solution)/shard_map/pallas_call | solution.py:235

commit v5 on v4

--- a/solution.py
+++ b/solution.py
@@ -9,7 +9,7 @@
 MESH = pl.DeviceIdType.MESH
 LONG, WIDE = 8, 4
 VLIM = 50 << 20
-GROUP = 4
+CUT = 40
 ROUNDS = LONG // 2 + WIDE // 2 - 1
 RANKED = {(LONG - 1, 0): 2.5, (LONG - 1, 1): 2, (LONG - 1, 2): 1.5}
 
@@ -211,20 +211,22 @@
     )(master, second, weight, gain)
 
 
-def finish_kernel(blocks, squares, routed, final, scale, serve, ready, inverse, sem):
+def finish_kernel(blocks, squares, routed, final, scale, serve, ready, root, sem):
     held, rows, width = squares.shape
     copies = [pltpu.make_async_copy(routed, serve, sem.at[0])]
     copies[0].start()
-    for e in range(held):
-        inverse[e] = jnp.broadcast_to(1.0 / jnp.sqrt(jnp.sum(squares[e], axis=1, keepdims=True)), (rows, width))
-    for start in range(0, blocks.shape[0], GROUP):
-        for shard in range(start, start + GROUP):
-            ready[:, :, shard * width:(shard + 1) * width] = (
-                blocks[shard].astype(jnp.float32) * inverse[...]).astype(jnp.bfloat16)
-        lanes = pl.ds(start * width, GROUP * width)
-        copies.append(pltpu.make_async_copy(ready.at[:, :, lanes], final.at[:, :, lanes], sem.at[len(copies)]))
+    for start in range(0, rows, CUT):
+        part = pl.ds(start, CUT)
+        total = jnp.sum(squares[:, part], axis=2, keepdims=True)
+        inverse = jnp.broadcast_to(1.0 / jnp.sqrt(total), (held, CUT, width))
+        for shard in range(blocks.shape[0]):
+            ready[:, part, shard * width:(shard + 1) * width] = (
+                blocks[shard, :, part].astype(jnp.float32) * inverse).astype(jnp.bfloat16)
+        copies.append(pltpu.make_async_copy(ready.at[:, part], final.at[:, part], sem.at[len(copies)]))
         copies[-1].start()
-    scale[...] = jnp.sqrt(jnp.stack([jnp.sum(jnp.swapaxes(squares[e], 0, 1), axis=0) for e in range(held)]))
+    root[...] = jnp.sqrt(jnp.stack([jnp.sum(jnp.swapaxes(squares[e], 0, 1), axis=0) for e in range(held)]))
+    copies.append(pltpu.make_async_copy(root, scale, sem.at[len(copies)]))
+    copies[-1].start()
     for copy in copies:
         copy.wait()
 
@@ -240,11 +242,11 @@
             jax.ShapeDtypeStruct(routed.shape, jnp.bfloat16),
         ),
         in_specs=[vmem, vmem, vmem],
-        out_specs=(hbm, vmem, hbm),
+        out_specs=(hbm, hbm, hbm),
         scratch_shapes=[
             pltpu.VMEM((held, rows, shards * width), jnp.bfloat16),
-            pltpu.VMEM((held, rows, width), jnp.float32),
-            pltpu.SemaphoreType.DMA((1 + shards // GROUP,)),
+            pltpu.VMEM((held, rows), jnp.float32),
+            pltpu.SemaphoreType.DMA((2 + rows // CUT,)),
         ],
         compiler_params=pltpu.CompilerParams(vmem_limit_bytes=VLIM),
     )(blocks, squares, routed)

time: 85 us -> 84.3 us (level)
  no operation moved by 1% of the time
where the time goes in v5:
time: 84.3 us; the launch traced here: 84.2 us
  Pallas kernels  83.6 us (99%)
    pallas_call x1, Pallas kernels, exchange(): pl.pallas_call(functools.partial(exchange_kernel, plan, experts), out_sha...  81.6 us
    pallas_call x1, Pallas kernels, finish(): pl.pallas_call(finish_kernel, out_shape=(jax.ShapeDtypeStruct((held, rows...  2.02 us

profile of v5, /device:TPU:64, one launch (start us, length us, event | category | flops | bytes accessed | tf_op | source)
XLA Modules:
  0.0 84.2 jit_solution(16254539134088842161)
XLA Ops:
  0.6 81.6 %shard_map.67 = (bf16[32,2,200,128]{3,2,1,0:T(8,128)(2,1)S(1)}, f32[2,200,128]{2,1,0:T(8,128)S(1)}, bf16[16,4096]{1,0:T(8,128)(2,1)S(1)}) custom-call(f32[2,32,200,128]{3,2,1,0:T(8,128)} %bitcast.5, bf16[2,32,200,128]{3,2,1,0:T(8,128)(2,1)} %bitcast.6, f32[2,128]{1,0:T(2,128)} %bitcast.7, f32[1,128]{1,0:T(1,128)} %bitcast.8), custom_call_target="tpu_custom_call" | custom-call | tf_op jit(solution)/shard_map/pallas_call | solution.py:191
  82.2 2.0 %shard_map.68 = (bf16[2,200,4096]{2,1,0:T(8,128)(2,1)}, f32[2,200]{1,0:T(2,128)}, bf16[16,4096]{1,0:T(8,128)(2,1)}) custom-call(bf16[32,2,200,128]{3,2,1,0:T(8,128)(2,1)S(1)} %get-tuple-element.9.blocks, f32[2,200,128]{2,1,0:T(8,128)S(1)} %get-tuple-element.10.squares, bf16[16,4096]{1,0:T(8,128)(2,1)S(1)} %get-tuple-element.11.routed), custom_call_target="tpu_custom_call" | custom-call | tf_op jit(solution)/shard_map/pallas_call | solution.py:237

commit v6 on v5

--- a/solution.py
+++ b/solution.py
@@ -10,6 +10,7 @@
 LONG, WIDE = 8, 4
 VLIM = 50 << 20
 CUT = 40
+FIRST = 8
 ROUNDS = LONG // 2 + WIDE // 2 - 1
 RANKED = {(LONG - 1, 0): 2.5, (LONG - 1, 1): 2, (LONG - 1, 2): 1.5}
 
@@ -27,7 +28,7 @@
             far = RANKED.get((z, target), min(along, LONG - along))
             other_half = z < LONG // 2 <= target and along != LONG // 2
             turned = (along > LONG // 2) != (across == WIDE - 1)
-            return other_half, -(far + 2 * min(across, WIDE - across)), -far, turned, across, along
+            return other_half, -(far + 1.75 * min(across, WIDE - across)), -far, turned, across, along
 
         return early + sorted((step for step in every if step not in early), key=key)
 
@@ -215,10 +216,10 @@
     held, rows, width = squares.shape
     copies = [pltpu.make_async_copy(routed, serve, sem.at[0])]
     copies[0].start()
-    for start in range(0, rows, CUT):
-        part = pl.ds(start, CUT)
+    for start, size in [(0, FIRST), (FIRST, CUT - FIRST)] + [(start, CUT) for start in range(CUT, rows, CUT)]:
+        part = pl.ds(start, size)
         total = jnp.sum(squares[:, part], axis=2, keepdims=True)
-        inverse = jnp.broadcast_to(1.0 / jnp.sqrt(total), (held, CUT, width))
+        inverse = jnp.broadcast_to(1.0 / jnp.sqrt(total), (held, size, width))
         for shard in range(blocks.shape[0]):
             ready[:, part, shard * width:(shard + 1) * width] = (
                 blocks[shard, :, part].astype(jnp.float32) * inverse).astype(jnp.bfloat16)
@@ -246,7 +247,7 @@
         scratch_shapes=[
             pltpu.VMEM((held, rows, shards * width), jnp.bfloat16),
             pltpu.VMEM((held, rows), jnp.float32),
-            pltpu.SemaphoreType.DMA((2 + rows // CUT,)),
+            pltpu.SemaphoreType.DMA((3 + rows // CUT,)),
         ],
         compiler_params=pltpu.CompilerParams(vmem_limit_bytes=VLIM),
     )(blocks, squares, routed)

time: 84.3 us -> 84.3 us (level)
  no operation moved by 1% of the time
where the time goes in v6:
time: 84.3 us; the launch traced here: 84.2 us
  Pallas kernels  83.5 us (99%)
    pallas_call x1, Pallas kernels, exchange(): pl.pallas_call(functools.partial(exchange_kernel, plan, experts), out_sha...  81.6 us
    pallas_call x1, Pallas kernels, finish(): pl.pallas_call(finish_kernel, out_shape=(jax.ShapeDtypeStruct((held, rows...  1.98 us

profile of v6, /device:TPU:64, one launch (start us, length us, event | category | flops | bytes accessed | tf_op | source)
XLA Modules:
  0.0 84.2 jit_solution(10266329731341679463)
XLA Ops:
  0.6 81.6 %shard_map.67 = (bf16[32,2,200,128]{3,2,1,0:T(8,128)(2,1)S(1)}, f32[2,200,128]{2,1,0:T(8,128)S(1)}, bf16[16,4096]{1,0:T(8,128)(2,1)S(1)}) custom-call(f32[2,32,200,128]{3,2,1,0:T(8,128)} %bitcast.5, bf16[2,32,200,128]{3,2,1,0:T(8,128)(2,1)} %bitcast.6, f32[2,128]{1,0:T(2,128)} %bitcast.7, f32[1,128]{1,0:T(1,128)} %bitcast.8), custom_call_target="tpu_custom_call" | custom-call | tf_op jit(solution)/shard_map/pallas_call | solution.py:192
  82.2 2.0 %shard_map.68 = (bf16[2,200,4096]{2,1,0:T(8,128)(2,1)}, f32[2,200]{1,0:T(2,128)}, bf16[16,4096]{1,0:T(8,128)(2,1)}) custom-call(bf16[32,2,200,128]{3,2,1,0:T(8,128)(2,1)S(1)} %get-tuple-element.9.blocks, f32[2,200,128]{2,1,0:T(8,128)S(1)} %get-tuple-element.10.squares, bf16[16,4096]{1,0:T(8,128)(2,1)S(1)} %get-tuple-element.11.routed), custom_call_target="tpu_custom_call" | custom-call | tf_op jit(solution)/shard_map/pallas_call | solution.py:238
